TPU v7x, 32 devices: a whole 2x2x4 slice. The times are simulated.
32 devices in a mesh: prow: 8 (over z, x), pcol: 4 (over y, core).
Axes of the slice: x: 2, y: 2, z: 4, core: 2. Of those that a mesh axis runs over, the one named last changes fastest.
Arguments:
- a_matrix: bfloat16 [32768, 512], P('prow', 'pcol'), may hold values from -6 to 6
- l_panel: bfloat16 [32768, 256], P('prow', 'pcol'), may hold values from -0.375 to 0.375
- l_inverse: bfloat16 [256, 256], replicated, may hold values from -1 to 1
- pivots: int32 [256], replicated, may hold values from 0 to 32767, as said below
Outputs:
- updated: bfloat16 [32768, 512], P('prow', 'pcol')
Inputs may be any that keep to these rules, and one draw needn't show every extreme that they name: pivots[j] >= j for every j.
All inputs are finite; a program needn't handle non-finite values.
Results may differ from a plain program's by a relative error of at most 0.0039.
Values may be sent and summed in bfloat16 or wider, within the bound.
A program may use at most 64 MiB of HBM per device.

v0:
```python
import jax
import jax.numpy as jnp
from jax import lax
from jax.sharding import PartitionSpec as P


def swap_plan(pivots, panel_width):
    slot_ids = jnp.arange(panel_width, dtype=jnp.int32)
    earlier = slot_ids[None, :] < slot_ids[:, None]
    hits = (pivots[None, :] == slot_ids[:, None]) & earlier
    pointer = jnp.max(jnp.where(hits, slot_ids[None, :], -1), axis=1)
    chain = jnp.where(pointer >= 0, pointer, slot_ids)
    for _ in range(panel_width.bit_length()):
        chain = jnp.take(chain, chain)
    same = pivots[None, :] == pivots[:, None]
    previous = jnp.max(jnp.where(same & earlier, slot_ids[None, :], -1), axis=1)
    top_source = jnp.where(previous >= 0, jnp.take(chain, jnp.maximum(previous, 0)), pivots)
    later = slot_ids[None, :] > slot_ids[:, None]
    is_last = jnp.logical_not(jnp.any(same & later, axis=1))
    return (top_source, chain, is_last)


def body(a_matrix, l_panel, l_inverse, pivots):
    local_count, col_count = a_matrix.shape
    panel_width = l_inverse.shape[0]
    prow_count = lax.axis_size("prow")
    prow_index = lax.axis_index("prow")
    top_source, moved_source, is_last = swap_plan(pivots, panel_width)
    local_rows = jnp.arange(local_count, dtype=jnp.int32)
    global_rows = (
        local_rows // panel_width * prow_count + prow_index
    ) * panel_width + local_rows % panel_width

    def owner_of(wanted):
        return wanted // panel_width % prow_count

    def local_of(wanted):
        return wanted // (panel_width * prow_count) * panel_width + wanted % panel_width

    def owned_part(wanted, usable):
        taken = jnp.take(a_matrix, local_of(wanted), axis=0).astype(jnp.float32)
        return jnp.where(
            ((owner_of(wanted) == prow_index) & usable)[:, None], taken, jnp.zeros((), jnp.float32)
        )

    usable_moves = is_last & (pivots >= panel_width)
    top_part = owned_part(top_source, jnp.ones((panel_width,), jnp.bool_))
    moved_part = owned_part(moved_source, usable_moves)
    moved_rows = lax.psum(moved_part, "prow")
    landing = jnp.where(
        usable_moves & (owner_of(pivots) == prow_index), local_of(pivots), local_count
    )
    swapped = a_matrix.at[landing].set(moved_rows.astype(jnp.bfloat16), mode="drop")
    top_rows = lax.psum(top_part, "prow")
    u_block = jnp.dot(
        l_inverse, top_rows.astype(jnp.bfloat16), preferred_element_type=jnp.float32
    ).astype(jnp.bfloat16)
    panel_full = lax.all_gather(l_panel, "pcol", axis=1, tiled=True)
    update = jnp.dot(panel_full, u_block, preferred_element_type=jnp.float32)
    updated = (swapped.astype(jnp.float32) - update).astype(jnp.bfloat16)
    u_padded = jnp.concatenate(
        [u_block, jnp.zeros((local_count - panel_width, col_count), jnp.bfloat16)], axis=0
    )
    return jnp.where((global_rows < panel_width)[:, None], u_padded, updated)


def solution(mesh):
    in_specs = (P("prow", "pcol"), P("prow", "pcol"), P(), P())
    out_specs = P("prow", "pcol")
    return jax.shard_map(body, mesh=mesh, in_specs=in_specs, out_specs=out_specs, check_vma=False)
```

profile of v0, /device:TPU:0, one launch (start us, length us, event | category | flops | bytes accessed | tf_op | source)
XLA Modules:
  0.0 115.9 jit_solution(2225911435671411788)
XLA Ops:
  7.4 0.0 copy-start
  7.4 0.0 copy-start.1
  7.4 0.0 all-reduce.4.cloned.1.call-start
  7.4 1.3 %copy.16 = bf16[4096,128]{1,0:T(8,128)(2,1)S(1)} copy(bf16[4096,128]{1,0:T(8,128)(2,1)} %param.8) | data formatting | bytes 2097152
  8.6 0.0 copy-done.1
  8.6 0.2 select_reduce_fusion
  8.9 0.2 fusion.4
  9.1 1.9 %gather_fusion = s32[256]{0:T(256)S(1)} fusion(s32[256]{0:T(256)S(1)} %get-tuple-element.34, s32[1024]{0:T(1024)S(1)} %pad_clamp_fusion.11), kind=kCustom, calls=%fused_computation.clone | custom fusion | bytes 3072 | tf_op jit(solution)/shard_map/jit(_take)/gather | solution.py:14
  11.0 1.9 %gather_fusion.1 = s32[256]{0:T(256)S(1)} fusion(s32[256]{0:T(256)S(1)} %get-tuple-element.32, s32[1024]{0:T(1024)S(1)} %pad_clamp_fusion.10), kind=kCustom, calls=%fused_computation.2.clone | custom fusion | bytes 3072 | tf_op jit(solution)/shard_map/jit(_take)/gather | solution.py:14
  13.0 1.9 %gather_fusion.2 = s32[256]{0:T(256)S(1)} fusion(s32[256]{0:T(256)S(1)} %get-tuple-element.30, s32[1024]{0:T(1024)S(1)} %pad_clamp_fusion.9), kind=kCustom, calls=%fused_computation.3.clone | custom fusion | bytes 3072 | tf_op jit(solution)/shard_map/jit(_take)/gather | solution.py:14
  15.0 1.9 %gather_fusion.3 = s32[256]{0:T(256)S(1)} fusion(s32[256]{0:T(256)S(1)} %get-tuple-element.28, s32[1024]{0:T(1024)S(1)} %pad_clamp_fusion.8), kind=kCustom, calls=%fused_computation.4.clone | custom fusion | bytes 3072 | tf_op jit(solution)/shard_map/jit(_take)/gather | solution.py:14
  17.0 1.9 %gather_fusion.4 = s32[256]{0:T(256)S(1)} fusion(s32[256]{0:T(256)S(1)} %get-tuple-element.26, s32[1024]{0:T(1024)S(1)} %pad_clamp_fusion.7), kind=kCustom, calls=%fused_computation.5.clone | custom fusion | bytes 3072 | tf_op jit(solution)/shard_map/jit(_take)/gather | solution.py:14
  19.0 1.9 %gather_fusion.5 = s32[256]{0:T(256)S(1)} fusion(s32[256]{0:T(256)S(1)} %get-tuple-element.24, s32[1024]{0:T(1024)S(1)} %pad_clamp_fusion.6), kind=kCustom, calls=%fused_computation.6.clone | custom fusion | bytes 3072 | tf_op jit(solution)/shard_map/jit(_take)/gather | solution.py:14
  21.0 1.9 %gather_fusion.6 = s32[256]{0:T(256)S(1)} fusion(s32[256]{0:T(256)S(1)} %get-tuple-element.22, s32[1024]{0:T(1024)S(1)} %pad_clamp_fusion.5), kind=kCustom, calls=%fused_computation.7.clone | custom fusion | bytes 3072 | tf_op jit(solution)/shard_map/jit(_take)/gather | solution.py:14
  23.0 1.9 %gather_fusion.7 = s32[256]{0:T(256)S(1)} fusion(s32[256]{0:T(256)S(1)} %get-tuple-element.20, s32[1024]{0:T(1024)S(1)} %pad_clamp_fusion.4), kind=kCustom, calls=%fused_computation.8.clone | custom fusion | bytes 3072 | tf_op jit(solution)/shard_map/jit(_take)/gather | solution.py:14
  25.0 1.9 %gather_fusion.8 = s32[256]{0:T(256)S(1)} fusion(s32[256]{0:T(256)S(1)} %get-tuple-element.18, s32[1024]{0:T(1024)S(1)} %pad_clamp_fusion.3), kind=kCustom, calls=%fused_computation.9.clone | custom fusion | bytes 3072 | tf_op jit(solution)/shard_map/jit(_take)/gather | solution.py:14
  27.0 0.9 gather_fusion.11
  27.8 0.8 convert_select_fusion
  28.6 0.0 all-reduce.4.cloned.1.call-update
  28.6 0.0 all-gather.2.cloned.1.call-start
  28.7 0.5 all-gather.2.cloned.1.call-update
  29.2 1.9 %gather_fusion.9 = s32[256]{0:T(256)S(1)} fusion(s32[256]{0:T(256)S(1)} %get-tuple-element.10, s32[1024]{0:T(1024)S(1)} %pad_clamp_fusion.2), kind=kCustom, calls=%fused_computation.10.clone | custom fusion | bytes 3072 | tf_op jit(solution)/shard_map/jit(_take)/gather | solution.py:17
  31.3 0.9 gather_fusion.10
  32.1 0.1 convert_select_fusion.1
  32.3 40.3 %all-reduce.5 = bf16[256,128]{1,0:T(8,128)(2,1)S(1)} all-reduce(f32[256,128]{1,0:T(8,128)S(1)} %convert_select_fusion.1), channel_id=1, replica_groups=mesh['prow'=8,'pcol'=4] {'prow'}, use_global_device_ids=true, to_apply=%region_2.5 | all-reduce | flops 32768 | bytes 196608 | tf_op jit(solution)/shard_map/psum | solution.py:54
  72.6 0.0 copy-done
  72.6 0.2 convolution_convert_fusion
  72.8 29.3 %all-reduce.4.cloned.1.call-done = f32[256,128]{1,0:T(8,128)} async-done(((f32[256,128]{1,0:T(8,128)}), f32[256,128]{1,0:T(8,128)}) %all-reduce.4.cloned.1.call-update) | async-done | bytes 131088 | tf_op jit(solution)/shard_map/psum | solution.py:49
  102.1 2.2 %scatter_custom_fusion = bf16[4096,128]{1,0:T(8,128)(2,1)S(1)} fusion(bf16[4096,128]{1,0:T(8,128)(2,1)S(1)} %copy.16, s32[256]{0:T(256)S(1)} %compare_select_fusion.11, f32[256,128]{1,0:T(8,128)} %all-reduce.4.cloned.1.call-done), kind=kCustom, calls=%fused_computation.29 | custom fusion | flops 32768 | bytes 1179648 | tf_op jit(solution)/shard_map/scatter | solution.py:53
  104.3 0.5 copy.9
  104.8 0.0 all-gather.2.cloned.1.call-done
  104.9 2.2 %fusion.2 = bf16[4096,128]{0,1:T(8,128)(2,1)S(1)} fusion(bf16[128,256]{1,0:T(8,128)(2,1)S(1)} %convolution_convert_fusion, bf16[4096,256]{0,1:T(8,128)(2,1)} %all-gather.2.cloned.1.call-done, bf16[4096,128]{0,1:T(8,128)(2,1)S(1)} %copy.9, bf16[256,128]{0,1:T(8,128)(2,1)S(1)} %bitcast.13, pred[4096]{0:T(1024)(128)(4,1)S(1)} %fusion.18), kind=kOutput, calls=%fused_computation.16 | convolution fusion | flops 270532608 | bytes 4329472 | tf_op jit(solution)/shard_map/dot_general | solution.py:59
  107.1 1.3 %copy.10 = bf16[4096,128]{1,0:T(8,128)(2,1)} copy(bf16[4096,128]{0,1:T(8,128)(2,1)S(1)} %fusion.2) | data formatting | bytes 2097152 | tf_op jit(solution)/shard_map/jit(_where)/select_n | solution.py:64
  (27 shorter events, 0.3 us)
Async XLA Ops:
  7.4 65.2 %copy-start = (bf16[256,256]{1,0:T(8,128)(2,1)S(1)}, bf16[256,256]{1,0:T(8,128)(2,1)}, u32[]{:S(2)}) copy-start(bf16[256,256]{1,0:T(8,128)(2,1)} %param.10) | copy-start | bytes 393220
  7.4 1.3 %copy-start.1 = (s32[256]{0:T(256)S(1)}, s32[256]{0:T(256)}, u32[]{:S(2)}) copy-start(s32[256]{0:T(256)} %param.11) | copy-start | bytes 3076
  7.4 94.8 %all-reduce.4.cloned.1.call-start = ((), (), s32[]{:S(2)}) async-start(), calls=%async_computation | async-start | bytes 262144 | tf_op jit(solution)/shard_map/psum | solution.py:49
  28.6 76.2 %all-gather.2.cloned.1.call-start = ((), (), s32[]{:S(2)}) async-start(), calls=%async_computation.1 | async-start | bytes 2621440 | tf_op jit(solution)/shard_map/all_gather | solution.py:58
Sparse Core Ops, SparseCore 0:
  28.8 73.3 all-reduce.3
Sparse Core Ops, SparseCore 1:
  30.7 25.1 all-gather.1
where the time goes:
time: 116 us
  blocking collectives  40.3 us (35%)
  waiting for transfers between devices  29.9 us (26%)
  local copies, waits for them, and re-layouts  24.3 us (21%)
  between operations  15.2 us (13%)
  other arithmetic  3.71 us (3%)
  matrix products  2.41 us (2%)
    psum x1, blocking collectives, body(): top_rows = lax.psum(top_part, 'prow')  40.3 us
    psum x1, waiting for transfers between devices, body(): moved_rows = lax.psum(moved_part, 'prow')  29.3 us
    gather x9, local copies, waits for them, and re-layouts, swap_plan(): chain = jnp.take(chain, chain)  17.6 us
  transfers between devices with their start and end apart: 2, of which 1 were waited for; matrix products, arithmetic and copies ran while one was open for 5% of the time, Pallas kernels for 0%

commit v1 on v0

--- a/solution.py
+++ b/solution.py
@@ -51,7 +51,7 @@
         usable_moves & (owner_of(pivots) == prow_index), local_of(pivots), local_count
     )
     swapped = a_matrix.at[landing].set(moved_rows.astype(jnp.bfloat16), mode="drop")
-    top_rows = lax.psum(top_part, "prow")
+    top_rows = jnp.sum(lax.all_gather(top_part, "prow"), axis=0)
     u_block = jnp.dot(
         l_inverse, top_rows.astype(jnp.bfloat16), preferred_element_type=jnp.float32
     ).astype(jnp.bfloat16)

time: 116 us -> 176 us (1.52)
  waiting for transfers between devices: 29.9 us -> 130 us
  blocking collectives: 40.3 us -> 0 us
  other arithmetic: 3.71 us -> 5.67 us
  between operations: 15.2 us -> 13.4 us
    psum x1 -> x0, blocking collectives: 40.3 us -> none  [body(): top_rows = lax.psum(top_part, 'prow')]
    psum x1, waiting for transfers between devices: 29.3 us -> 68.9 us  [body(): moved_rows = lax.psum(moved_part, 'prow')]
    all_gather x0 -> x1, waiting for transfers between devices: none -> 38.8 us  [body(): top_rows = jnp.sum(lax.all_gather(top_part, 'prow'), axis=0)]
    all_gather x1, waiting for transfers between devices: 0.03 us -> 21.4 us  [body(): panel_full = lax.all_gather(l_panel, 'pcol', axis=1, tiled=True)]
  transfers between devices with their start and end apart: 2 -> 3, of which waited for: 1 -> 3; matrix products, arithmetic and copies ran while one was open for 5% -> 4% of each run, Pallas kernels for 0% -> 0%
where the time goes in v1:
time: 176 us
  waiting for transfers between devices  130 us (74%)
  local copies, waits for them, and re-layouts  24.3 us (14%)
  between operations  13.4 us (8%)
  other arithmetic  5.67 us (3%)
  matrix products  2.35 us (1%)
    psum x1, waiting for transfers between devices, body(): moved_rows = lax.psum(moved_part, 'prow')  68.9 us
    all_gather x1, waiting for transfers between devices, body(): top_rows = jnp.sum(lax.all_gather(top_part, 'prow'), axis=0)  38.8 us
    all_gather x1, waiting for transfers between devices, body(): panel_full = lax.all_gather(l_panel, 'pcol', axis=1, tiled=True)  21.4 us
    gather x9, local copies, waits for them, and re-layouts, swap_plan(): chain = jnp.take(chain, chain)  17.5 us
  transfers between devices with their start and end apart: 3, of which 3 were waited for; matrix products, arithmetic and copies ran while one was open for 4% of the time, Pallas kernels for 0%

profile of v1, /device:TPU:0, one launch (start us, length us, event | category | flops | bytes accessed | tf_op | source)
XLA Modules:
  0.0 175.6 jit_solution(107831242290496003)
XLA Ops:
  6.5 0.0 copy-start
  6.5 0.0 copy-start.1
  6.5 0.0 all-reduce.3.cloned.1.call-start
  6.5 1.3 copy.14
  7.8 0.0 copy-done.1
  7.8 0.2 select_reduce_fusion
  8.0 0.2 fusion.4
  8.2 1.9 %gather_fusion = s32[256]{0:T(256)S(1)} fusion(s32[256]{0:T(256)S(1)} %get-tuple-element.34, s32[1024]{0:T(1024)S(1)} %pad_clamp_fusion.11), kind=kCustom, calls=%fused_computation.clone | custom fusion | bytes 3072 | tf_op jit(solution)/shard_map/jit(_take)/gather | solution.py:14
  10.2 1.9 %gather_fusion.1 = s32[256]{0:T(256)S(1)} fusion(s32[256]{0:T(256)S(1)} %get-tuple-element.32, s32[1024]{0:T(1024)S(1)} %pad_clamp_fusion.10), kind=kCustom, calls=%fused_computation.2.clone | custom fusion | bytes 3072 | tf_op jit(solution)/shard_map/jit(_take)/gather | solution.py:14
  12.2 1.9 %gather_fusion.2 = s32[256]{0:T(256)S(1)} fusion(s32[256]{0:T(256)S(1)} %get-tuple-element.30, s32[1024]{0:T(1024)S(1)} %pad_clamp_fusion.9), kind=kCustom, calls=%fused_computation.3.clone | custom fusion | bytes 3072 | tf_op jit(solution)/shard_map/jit(_take)/gather | solution.py:14
  14.2 1.9 %gather_fusion.3 = s32[256]{0:T(256)S(1)} fusion(s32[256]{0:T(256)S(1)} %get-tuple-element.28, s32[1024]{0:T(1024)S(1)} %pad_clamp_fusion.8), kind=kCustom, calls=%fused_computation.4.clone | custom fusion | bytes 3072 | tf_op jit(solution)/shard_map/jit(_take)/gather | solution.py:14
  16.1 1.9 %gather_fusion.4 = s32[256]{0:T(256)S(1)} fusion(s32[256]{0:T(256)S(1)} %get-tuple-element.26, s32[1024]{0:T(1024)S(1)} %pad_clamp_fusion.7), kind=kCustom, calls=%fused_computation.5.clone | custom fusion | bytes 3072 | tf_op jit(solution)/shard_map/jit(_take)/gather | solution.py:14
  18.1 1.9 %gather_fusion.5 = s32[256]{0:T(256)S(1)} fusion(s32[256]{0:T(256)S(1)} %get-tuple-element.24, s32[1024]{0:T(1024)S(1)} %pad_clamp_fusion.6), kind=kCustom, calls=%fused_computation.6.clone | custom fusion | bytes 3072 | tf_op jit(solution)/shard_map/jit(_take)/gather | solution.py:14
  20.1 1.9 %gather_fusion.6 = s32[256]{0:T(256)S(1)} fusion(s32[256]{0:T(256)S(1)} %get-tuple-element.22, s32[1024]{0:T(1024)S(1)} %pad_clamp_fusion.5), kind=kCustom, calls=%fused_computation.7.clone | custom fusion | bytes 3072 | tf_op jit(solution)/shard_map/jit(_take)/gather | solution.py:14
  22.1 1.9 %gather_fusion.7 = s32[256]{0:T(256)S(1)} fusion(s32[256]{0:T(256)S(1)} %get-tuple-element.20, s32[1024]{0:T(1024)S(1)} %pad_clamp_fusion.4), kind=kCustom, calls=%fused_computation.8.clone | custom fusion | bytes 3072 | tf_op jit(solution)/shard_map/jit(_take)/gather | solution.py:14
  24.1 1.9 %gather_fusion.8 = s32[256]{0:T(256)S(1)} fusion(s32[256]{0:T(256)S(1)} %get-tuple-element.18, s32[1024]{0:T(1024)S(1)} %pad_clamp_fusion.3), kind=kCustom, calls=%fused_computation.9.clone | custom fusion | bytes 3072 | tf_op jit(solution)/shard_map/jit(_take)/gather | solution.py:14
  26.1 0.9 gather_fusion.11
  26.9 0.8 convert_select_fusion
  27.7 0.0 all-reduce.3.cloned.1.call-update
  27.8 0.0 all-gather.6.cloned.1.call-start
  27.8 1.9 %gather_fusion.9 = s32[256]{0:T(256)S(1)} fusion(s32[256]{0:T(256)S(1)} %get-tuple-element.10, s32[1024]{0:T(1024)S(1)} %pad_clamp_fusion.2), kind=kCustom, calls=%fused_computation.10.clone | custom fusion | bytes 3072 | tf_op jit(solution)/shard_map/jit(_take)/gather | solution.py:17
  29.8 0.9 gather_fusion.10
  30.7 0.8 convert_select_fusion.1
  31.5 0.0 all-gather.6.cloned.1.call-update
  31.5 0.0 all-gather.4.cloned.1.call-start
  31.6 0.7 all-gather.4.cloned.1.call-update
  32.3 68.9 %all-reduce.3.cloned.1.call-done = f32[256,128]{1,0:T(8,128)} async-done(((f32[256,128]{1,0:T(8,128)}), f32[256,128]{1,0:T(8,128)}) %all-reduce.3.cloned.1.call-update) | async-done | bytes 131088 | tf_op jit(solution)/shard_map/psum | solution.py:49
  101.2 2.2 %scatter_custom_fusion = bf16[4096,128]{1,0:T(8,128)(2,1)S(1)} fusion(bf16[4096,128]{1,0:T(8,128)(2,1)S(1)} %copy.14, s32[256]{0:T(256)S(1)} %compare_select_fusion.11, f32[256,128]{1,0:T(8,128)} %all-reduce.3.cloned.1.call-done), kind=kCustom, calls=%fused_computation.29 | custom fusion | flops 32768 | bytes 1179648 | tf_op jit(solution)/shard_map/scatter | solution.py:53
  103.3 0.5 copy.9
  103.9 38.8 %all-gather.6.cloned.1.call-done = f32[2048,128]{1,0:T(8,128)} async-done(((f32[256,128]{1,0:T(8,128)}), f32[2048,128]{1,0:T(8,128)}) %all-gather.6.cloned.1.call-update) | async-done | bytes 1048592 | tf_op jit(solution)/shard_map/all_gather | solution.py:54
  142.7 1.3 reduce_sum.9
  144.0 0.0 copy-done
  144.0 0.2 convolution_convert_fusion
  144.2 21.4 %all-gather.4.cloned.1.call-done = bf16[4096,256]{0,1:T(8,128)(2,1)} async-done(((bf16[4096,64]{0,1:T(8,128)(2,1)}), bf16[4096,256]{0,1:T(8,128)(2,1)}) %all-gather.4.cloned.1.call-update) | async-done | bytes 2097168 | tf_op jit(solution)/shard_map/all_gather | solution.py:58
  165.6 2.2 %fusion.2 = bf16[4096,128]{0,1:T(8,128)(2,1)S(1)} fusion(bf16[128,256]{1,0:T(8,128)(2,1)S(1)} %convolution_convert_fusion, bf16[4096,256]{0,1:T(8,128)(2,1)} %all-gather.4.cloned.1.call-done, bf16[4096,128]{0,1:T(8,128)(2,1)S(1)} %copy.9, bf16[256,128]{0,1:T(8,128)(2,1)S(1)} %bitcast.15, pred[4096]{0:T(1024)(128)(4,1)S(1)} %fusion.18), kind=kOutput, calls=%fused_computation.16 | convolution fusion | flops 270532608 | bytes 4329472 | tf_op jit(solution)/shard_map/dot_general | solution.py:59
  167.7 1.3 copy.10
  (27 shorter events, 0.3 us)
Async XLA Ops:
  6.5 137.4 %copy-start = (bf16[256,256]{1,0:T(8,128)(2,1)S(1)}, bf16[256,256]{1,0:T(8,128)(2,1)}, u32[]{:S(2)}) copy-start(bf16[256,256]{1,0:T(8,128)(2,1)} %param.10) | copy-start | bytes 393220
  6.5 1.3 copy-start.1
  6.5 94.6 %all-reduce.3.cloned.1.call-start = ((), (), s32[]{:S(2)}) async-start(), calls=%async_computation | async-start | bytes 262144 | tf_op jit(solution)/shard_map/psum | solution.py:49
  27.8 114.9 %all-gather.6.cloned.1.call-start = ((), (), s32[]{:S(2)}) async-start(), calls=%async_computation.2 | async-start | bytes 1179648 | tf_op jit(solution)/shard_map/all_gather | solution.py:54
  31.5 134.0 %all-gather.4.cloned.1.call-start = ((), (), s32[]{:S(2)}) async-start(), calls=%async_computation.1 | async-start | bytes 2621440 | tf_op jit(solution)/shard_map/all_gather | solution.py:58
Sparse Core Ops, SparseCore 0:
  27.9 73.2 all-reduce.2
  103.3 39.3 all-gather.5
  144.3 21.2 all-gather.3
